TPU v7x, 32 devices: a whole 2x2x4 slice. The times are simulated.
32 devices in a mesh: groups: 2 (over x), blk: 16 (over z, y, core).
Axes of the slice: x: 2, y: 2, z: 4, core: 2. Of those that a mesh axis runs over, the one named last changes fastest.
Arguments:
- snapshots: bfloat16 [2, 65536, 2, 64], P('groups', 'blk'), parts along dimension 0, may hold values from -6 to 6
- bin_index: int32 [2], P('groups'), parts along dimension 0, may hold values from 1 to 4095
- positions: int32 [3, 65536], replicated, may hold values from 0 to 511
- directions: int32 [3, 4096], replicated, may hold values from -128 to 127
- taper: float32 [65536], replicated, may hold values from 0.5 to 2
- beam_order: int32 [4096], replicated, may hold values from 0 to 4095, each once
Outputs:
- beams: bfloat16 [4096, 2, 2, 64], P('blk', 'groups'), parts along dimension 1
There are 2 independent parts, one for each index of `groups`. A program takes and returns all parts, laid end to end along the dimension named above; an argument that names none is the same for every part. Nothing has to cross between parts.
Inputs may be any that keep to these rules, and one draw needn't show every extreme that they name: beam_order is a permutation of the 4096 beams.
All inputs are finite; a program needn't handle non-finite values.
Results may differ from a plain program's by a relative error of at most 0.0048.
Values may be sent and summed in bfloat16 or wider, within the bound.
A program may use at most 64 MiB of HBM per device.

v0:
```python
import math

import jax
import jax.numpy as jnp
from jax import lax
from jax.sharding import PartitionSpec as P

ELEM = 65536
CYCLE = 8192


def weight_block(dir_cols, positions, taper, bin_value):
    delays = dir_cols[0][:, None] * positions[0][None, :]
    delays = delays + dir_cols[1][:, None] * positions[1][None, :]
    delays = delays + dir_cols[2][:, None] * positions[2][None, :]
    delays = jnp.remainder(delays, CYCLE)
    phases = jnp.remainder(bin_value * delays, CYCLE)
    angles = phases.astype(jnp.float32) * (2.0 * math.pi / CYCLE)
    amplitude = taper / math.sqrt(ELEM)
    weight_re = (amplitude[None, :] * jnp.cos(angles)).astype(jnp.bfloat16)
    weight_im = (-amplitude[None, :] * jnp.sin(angles)).astype(jnp.bfloat16)
    return (weight_re, weight_im)


def beam_terms(dir_cols, positions, taper, snaps, bin_index):
    weight_re, weight_im = weight_block(dir_cols, positions, taper, bin_index[0])
    width = snaps.shape[3]
    columns = snaps[0].reshape(snaps.shape[1], 2 * width)
    with_real = jnp.dot(weight_re, columns, preferred_element_type=jnp.float32)
    with_imag = jnp.dot(weight_im, columns, preferred_element_type=jnp.float32)
    real_part = with_real[:, :width] - with_imag[:, width:]
    imag_part = with_real[:, width:] + with_imag[:, :width]
    results = [jnp.stack([real_part, imag_part], axis=1)]
    return jnp.stack(results, axis=1)


def blocked_terms(dir_cols, positions, taper, snaps, bin_index, row_block):
    count = dir_cols.shape[1]
    block_count = count // row_block
    blocks = dir_cols.reshape(3, block_count, row_block).transpose(1, 0, 2)

    def per_block(block_cols):
        return beam_terms(block_cols, positions, taper, snaps, bin_index)

    result = lax.map(per_block, blocks)
    return result.reshape(count, snaps.shape[0], 2, snaps.shape[3])


def per_device(snapshots, bin_index, positions, directions, taper, beam_order):
    ordered = jnp.take(directions, beam_order, axis=1)
    local_count = snapshots.shape[1]
    index = lax.axis_index("blk")
    offset = index * local_count
    local_positions = lax.dynamic_slice_in_dim(positions, offset, local_count, 1)
    local_taper = lax.dynamic_slice_in_dim(taper, offset, local_count, 0)
    owned_rows = ordered.shape[1] // lax.axis_size("blk")
    row_block = math.gcd(owned_rows * lax.axis_size("blk"), 512)
    summed = lax.psum_scatter(
        blocked_terms(ordered, local_positions, local_taper, snapshots, bin_index, row_block),
        "blk",
        scatter_dimension=0,
        tiled=True,
    )
    return summed.astype(jnp.bfloat16)


def solution(mesh):
    in_specs = (P("groups", "blk", None, None), P("groups"), P(), P(), P(), P())
    out_specs = P("blk", "groups", None, None)
    return jax.shard_map(
        per_device, mesh=mesh, in_specs=in_specs, out_specs=out_specs, check_vma=False
    )
```

profile of v0, /device:TPU:0, one launch (start us, length us, event | category | flops | bytes accessed | tf_op | source)
XLA Modules:
  0.0 767.9 jit_solution(15803275848350345564)
XLA Ops:
  11.0 15.7 %gather_fusion = s32[4096,3]{1,0:T(8,128)} fusion(s32[3,4096]{0,1:T(8,128)} %copy.7, s32[4096]{0:T(1024)S(1)} %fusion.22), kind=kCustom, calls=%fused_computation | custom fusion | bytes 114688 | tf_op jit(solution)/shard_map/jit(_take)/gather | solution.py:50
  29.0 663.2 %while.12 = (s32[]{:T(128)}, f32[8,512,1,2,64]{1,0,4,3,2:T(8,128)}, f32[4096]{0:T(1024)S(1)}, s32[1]{0:T(128)}, s32[8,3,512]{2,1,0:T(4,128)S(1)}, /*index=5*/s32...) while((s32[]{:T(128)}, f32[8,512,1,2,64]{1,0,4,3,2:T(8,128)}, ...), condition=%wide.region_1.2_spmd, body=%wide.region_0.1_spmd.sunk | while | flops 1208098816 | bytes 22061212 | solution.py:45
  29.1 36.4 %multiply_convert_fusion.13 = bf16[512,4096]{1,0:T(8,128)(2,1)S(1)} fusion(s32[4096]{0:T(1024)S(1)} %bitcast.61, s32[512]{0:T(512)S(1)} %bitcast.70, s32[4096]{0:T(1024)S(1)} %bitcast.63, s32[512]{0:T(512)S(1)} %bitcast.68, s32[4096]{0:T(1024)S(1)} %bitcast.59, s32[512]{0:T(512)S(1)} %bitcast.66, s32[]{:T(128)} %bitcast.56, ...), kind=kLoop, calls=%fused_computation.13.clone.clone.1.clone.1 | loop fusion | flops 67108864 | bytes 4265988 | tf_op jit(solution)/shard_map/while/body/eval_jaxpr/dot_general | solution.py:29
  67.0 36.6 %multiply_convert_fusion.12 = bf16[512,4096]{1,0:T(8,128)(2,1)S(1)} fusion(f32[4096]{0:T(1024)S(1)} %get-tuple-element.173, s32[4096]{0:T(1024)S(1)} %bitcast.62, s32[512]{0:T(512)S(1)} %bitcast.71, s32[4096]{0:T(1024)S(1)} %bitcast.64, s32[512]{0:T(512)S(1)} %bitcast.69, s32[4096]{0:T(1024)S(1)} %bitcast.60, s32[512]{0:T(512)S(1)} %bitcast.67, ...), kind=kLoop, calls=%fused_computation.12.clone.clone.1.clone.1 | loop fusion | flops 67108864 | bytes 4265988 | tf_op jit(solution)/shard_map/while/body/eval_jaxpr/dot_general | solution.py:30
  105.5 6.3 dynamic_update_slice.8
  112.0 36.4 %multiply_convert_fusion.13 = bf16[512,4096]{1,0:T(8,128)(2,1)S(1)} fusion(s32[4096]{0:T(1024)S(1)} %bitcast.61, s32[512]{0:T(512)S(1)} %bitcast.70, s32[4096]{0:T(1024)S(1)} %bitcast.63, s32[512]{0:T(512)S(1)} %bitcast.68, s32[4096]{0:T(1024)S(1)} %bitcast.59, s32[512]{0:T(512)S(1)} %bitcast.66, s32[]{:T(128)} %bitcast.56, ...), kind=kLoop, calls=%fused_computation.13.clone.clone.1.clone.1 | loop fusion | flops 67108864 | bytes 4265988 | tf_op jit(solution)/shard_map/while/body/eval_jaxpr/dot_general | solution.py:29
  149.9 36.6 %multiply_convert_fusion.12 = bf16[512,4096]{1,0:T(8,128)(2,1)S(1)} fusion(f32[4096]{0:T(1024)S(1)} %get-tuple-element.173, s32[4096]{0:T(1024)S(1)} %bitcast.62, s32[512]{0:T(512)S(1)} %bitcast.71, s32[4096]{0:T(1024)S(1)} %bitcast.64, s32[512]{0:T(512)S(1)} %bitcast.69, s32[4096]{0:T(1024)S(1)} %bitcast.60, s32[512]{0:T(512)S(1)} %bitcast.67, ...), kind=kLoop, calls=%fused_computation.12.clone.clone.1.clone.1 | loop fusion | flops 67108864 | bytes 4265988 | tf_op jit(solution)/shard_map/while/body/eval_jaxpr/dot_general | solution.py:30
  188.4 6.3 dynamic_update_slice.8
  194.8 36.4 %multiply_convert_fusion.13 = bf16[512,4096]{1,0:T(8,128)(2,1)S(1)} fusion(s32[4096]{0:T(1024)S(1)} %bitcast.61, s32[512]{0:T(512)S(1)} %bitcast.70, s32[4096]{0:T(1024)S(1)} %bitcast.63, s32[512]{0:T(512)S(1)} %bitcast.68, s32[4096]{0:T(1024)S(1)} %bitcast.59, s32[512]{0:T(512)S(1)} %bitcast.66, s32[]{:T(128)} %bitcast.56, ...), kind=kLoop, calls=%fused_computation.13.clone.clone.1.clone.1 | loop fusion | flops 67108864 | bytes 4265988 | tf_op jit(solution)/shard_map/while/body/eval_jaxpr/dot_general | solution.py:29
  232.8 36.6 %multiply_convert_fusion.12 = bf16[512,4096]{1,0:T(8,128)(2,1)S(1)} fusion(f32[4096]{0:T(1024)S(1)} %get-tuple-element.173, s32[4096]{0:T(1024)S(1)} %bitcast.62, s32[512]{0:T(512)S(1)} %bitcast.71, s32[4096]{0:T(1024)S(1)} %bitcast.64, s32[512]{0:T(512)S(1)} %bitcast.69, s32[4096]{0:T(1024)S(1)} %bitcast.60, s32[512]{0:T(512)S(1)} %bitcast.67, ...), kind=kLoop, calls=%fused_computation.12.clone.clone.1.clone.1 | loop fusion | flops 67108864 | bytes 4265988 | tf_op jit(solution)/shard_map/while/body/eval_jaxpr/dot_general | solution.py:30
  271.3 6.3 dynamic_update_slice.8
  277.7 36.4 %multiply_convert_fusion.13 = bf16[512,4096]{1,0:T(8,128)(2,1)S(1)} fusion(s32[4096]{0:T(1024)S(1)} %bitcast.61, s32[512]{0:T(512)S(1)} %bitcast.70, s32[4096]{0:T(1024)S(1)} %bitcast.63, s32[512]{0:T(512)S(1)} %bitcast.68, s32[4096]{0:T(1024)S(1)} %bitcast.59, s32[512]{0:T(512)S(1)} %bitcast.66, s32[]{:T(128)} %bitcast.56, ...), kind=kLoop, calls=%fused_computation.13.clone.clone.1.clone.1 | loop fusion | flops 67108864 | bytes 4265988 | tf_op jit(solution)/shard_map/while/body/eval_jaxpr/dot_general | solution.py:29
  315.7 36.6 %multiply_convert_fusion.12 = bf16[512,4096]{1,0:T(8,128)(2,1)S(1)} fusion(f32[4096]{0:T(1024)S(1)} %get-tuple-element.173, s32[4096]{0:T(1024)S(1)} %bitcast.62, s32[512]{0:T(512)S(1)} %bitcast.71, s32[4096]{0:T(1024)S(1)} %bitcast.64, s32[512]{0:T(512)S(1)} %bitcast.69, s32[4096]{0:T(1024)S(1)} %bitcast.60, s32[512]{0:T(512)S(1)} %bitcast.67, ...), kind=kLoop, calls=%fused_computation.12.clone.clone.1.clone.1 | loop fusion | flops 67108864 | bytes 4265988 | tf_op jit(solution)/shard_map/while/body/eval_jaxpr/dot_general | solution.py:30
  354.2 6.3 dynamic_update_slice.8
  360.6 36.4 %multiply_convert_fusion.13 = bf16[512,4096]{1,0:T(8,128)(2,1)S(1)} fusion(s32[4096]{0:T(1024)S(1)} %bitcast.61, s32[512]{0:T(512)S(1)} %bitcast.70, s32[4096]{0:T(1024)S(1)} %bitcast.63, s32[512]{0:T(512)S(1)} %bitcast.68, s32[4096]{0:T(1024)S(1)} %bitcast.59, s32[512]{0:T(512)S(1)} %bitcast.66, s32[]{:T(128)} %bitcast.56, ...), kind=kLoop, calls=%fused_computation.13.clone.clone.1.clone.1 | loop fusion | flops 67108864 | bytes 4265988 | tf_op jit(solution)/shard_map/while/body/eval_jaxpr/dot_general | solution.py:29
  398.6 36.6 %multiply_convert_fusion.12 = bf16[512,4096]{1,0:T(8,128)(2,1)S(1)} fusion(f32[4096]{0:T(1024)S(1)} %get-tuple-element.173, s32[4096]{0:T(1024)S(1)} %bitcast.62, s32[512]{0:T(512)S(1)} %bitcast.71, s32[4096]{0:T(1024)S(1)} %bitcast.64, s32[512]{0:T(512)S(1)} %bitcast.69, s32[4096]{0:T(1024)S(1)} %bitcast.60, s32[512]{0:T(512)S(1)} %bitcast.67, ...), kind=kLoop, calls=%fused_computation.12.clone.clone.1.clone.1 | loop fusion | flops 67108864 | bytes 4265988 | tf_op jit(solution)/shard_map/while/body/eval_jaxpr/dot_general | solution.py:30
  437.1 6.3 dynamic_update_slice.8
  443.5 36.4 %multiply_convert_fusion.13 = bf16[512,4096]{1,0:T(8,128)(2,1)S(1)} fusion(s32[4096]{0:T(1024)S(1)} %bitcast.61, s32[512]{0:T(512)S(1)} %bitcast.70, s32[4096]{0:T(1024)S(1)} %bitcast.63, s32[512]{0:T(512)S(1)} %bitcast.68, s32[4096]{0:T(1024)S(1)} %bitcast.59, s32[512]{0:T(512)S(1)} %bitcast.66, s32[]{:T(128)} %bitcast.56, ...), kind=kLoop, calls=%fused_computation.13.clone.clone.1.clone.1 | loop fusion | flops 67108864 | bytes 4265988 | tf_op jit(solution)/shard_map/while/body/eval_jaxpr/dot_general | solution.py:29
  481.5 36.6 %multiply_convert_fusion.12 = bf16[512,4096]{1,0:T(8,128)(2,1)S(1)} fusion(f32[4096]{0:T(1024)S(1)} %get-tuple-element.173, s32[4096]{0:T(1024)S(1)} %bitcast.62, s32[512]{0:T(512)S(1)} %bitcast.71, s32[4096]{0:T(1024)S(1)} %bitcast.64, s32[512]{0:T(512)S(1)} %bitcast.69, s32[4096]{0:T(1024)S(1)} %bitcast.60, s32[512]{0:T(512)S(1)} %bitcast.67, ...), kind=kLoop, calls=%fused_computation.12.clone.clone.1.clone.1 | loop fusion | flops 67108864 | bytes 4265988 | tf_op jit(solution)/shard_map/while/body/eval_jaxpr/dot_general | solution.py:30
  526.4 36.4 %multiply_convert_fusion.13 = bf16[512,4096]{1,0:T(8,128)(2,1)S(1)} fusion(s32[4096]{0:T(1024)S(1)} %bitcast.61, s32[512]{0:T(512)S(1)} %bitcast.70, s32[4096]{0:T(1024)S(1)} %bitcast.63, s32[512]{0:T(512)S(1)} %bitcast.68, s32[4096]{0:T(1024)S(1)} %bitcast.59, s32[512]{0:T(512)S(1)} %bitcast.66, s32[]{:T(128)} %bitcast.56, ...), kind=kLoop, calls=%fused_computation.13.clone.clone.1.clone.1 | loop fusion | flops 67108864 | bytes 4265988 | tf_op jit(solution)/shard_map/while/body/eval_jaxpr/dot_general | solution.py:29
  564.4 36.6 %multiply_convert_fusion.12 = bf16[512,4096]{1,0:T(8,128)(2,1)S(1)} fusion(f32[4096]{0:T(1024)S(1)} %get-tuple-element.173, s32[4096]{0:T(1024)S(1)} %bitcast.62, s32[512]{0:T(512)S(1)} %bitcast.71, s32[4096]{0:T(1024)S(1)} %bitcast.64, s32[512]{0:T(512)S(1)} %bitcast.69, s32[4096]{0:T(1024)S(1)} %bitcast.60, s32[512]{0:T(512)S(1)} %bitcast.67, ...), kind=kLoop, calls=%fused_computation.12.clone.clone.1.clone.1 | loop fusion | flops 67108864 | bytes 4265988 | tf_op jit(solution)/shard_map/while/body/eval_jaxpr/dot_general | solution.py:30
  609.3 36.4 %multiply_convert_fusion.13 = bf16[512,4096]{1,0:T(8,128)(2,1)S(1)} fusion(s32[4096]{0:T(1024)S(1)} %bitcast.61, s32[512]{0:T(512)S(1)} %bitcast.70, s32[4096]{0:T(1024)S(1)} %bitcast.63, s32[512]{0:T(512)S(1)} %bitcast.68, s32[4096]{0:T(1024)S(1)} %bitcast.59, s32[512]{0:T(512)S(1)} %bitcast.66, s32[]{:T(128)} %bitcast.56, ...), kind=kLoop, calls=%fused_computation.13.clone.clone.1.clone.1 | loop fusion | flops 67108864 | bytes 4265988 | tf_op jit(solution)/shard_map/while/body/eval_jaxpr/dot_general | solution.py:29
  647.3 36.6 %multiply_convert_fusion.12 = bf16[512,4096]{1,0:T(8,128)(2,1)S(1)} fusion(f32[4096]{0:T(1024)S(1)} %get-tuple-element.173, s32[4096]{0:T(1024)S(1)} %bitcast.62, s32[512]{0:T(512)S(1)} %bitcast.71, s32[4096]{0:T(1024)S(1)} %bitcast.64, s32[512]{0:T(512)S(1)} %bitcast.69, s32[4096]{0:T(1024)S(1)} %bitcast.60, s32[512]{0:T(512)S(1)} %bitcast.67, ...), kind=kLoop, calls=%fused_computation.12.clone.clone.1.clone.1 | loop fusion | flops 67108864 | bytes 4265988 | tf_op jit(solution)/shard_map/while/body/eval_jaxpr/dot_general | solution.py:30
  694.9 64.7 %reduce-scatter.2.cloned.1.call-done = f32[256,1,2,64]{0,3,2,1:T(8,128)} async-done(((f32[4096,1,2,64]{0,3,2,1:T(8,128)}), f32[256,1,2,64]{0,3,2,1:T(8,128)}) %reduce-scatter.2.cloned.1.call-update) | async-done | bytes 131088 | tf_op jit(solution)/shard_map/reduce_scatter | solution.py:58
  (85 shorter events, 58.4 us)
Async XLA Ops:
  6.5 1.6 copy-start
  6.5 22.4 %copy-start.1 = (bf16[1,4096,2,64]{1,3,2,0:T(8,128)(2,1)S(1)}, bf16[1,4096,2,64]{1,3,2,0:T(8,128)(2,1)}, u32[]{:S(2)}) copy-start(bf16[1,4096,2,64]{1,3,2,0:T(8,128)(2,1)} %param.8) | copy-start | bytes 3145732
  6.5 753.0 %reduce-scatter.2.cloned.1.call-start = ((), (), s32[]{:S(2)}) async-start(), calls=%async_computation.1 | async-start | bytes 2228224 | tf_op jit(solution)/shard_map/reduce_scatter | solution.py:58
  8.1 20.8 %dynamic-slice-start = ((f32[65536]{0:T(1024)}, s32[]{:T(128)}), f32[4096]{0:T(1024)S(1)}, s32[]{:S(2)}) async-start(f32[65536]{0:T(1024)} %param.12, s32[]{:T(128)} %select_n.33), calls=%async_computation.2 | async-start | bytes 33280 | tf_op jit(solution)/shard_map/dynamic_slice | solution.py:55
Sparse Core Ops, SparseCore 0:
  695.0 64.4 reduce-scatter.1
where the time goes:
time: 769 us; the launch traced here: 768 us
  other arithmetic  587 us (76%)
  local copies, waits for them, and re-layouts  76.8 us (10%)
  waiting for transfers between devices  64.7 us (8%)
  matrix products  25.3 us (3%)
  between operations  13.4 us (2%)
    dot_general x8, other arithmetic, beam_terms(): with_imag = jnp.dot(weight_im, columns, preferred_element_type=jnp.float32)  292 us
    dot_general x8, other arithmetic, beam_terms(): with_real = jnp.dot(weight_re, columns, preferred_element_type=jnp.float32)  291 us
    reduce_scatter x1, waiting for transfers between devices, per_device(): lax.psum_scatter(blocked_terms(ordered, local_positions, local_taper, sna...  64.7 us
    dynamic_update_slice x16, local copies, waits for them, and re-layouts, blocked_terms(): result = lax.map(per_block, blocks)  52.9 us
    gather x2, local copies, waits for them, and re-layouts, per_device(): ordered = jnp.take(directions, beam_order, axis=1)  17.9 us
  transfers between devices with their start and end apart: 1, of which 1 were waited for; matrix products, arithmetic and copies ran while one was open for 0% of the time, Pallas kernels for 0%

commit v1 on v0

v1 whole, which is shorter than its diff:
```python
import functools
import math

import jax
import jax.numpy as jnp
from jax import lax
from jax.experimental import pallas as pl
from jax.experimental.pallas import tpu as pltpu
from jax.sharding import PartitionSpec as P

CYCLE = 8192
FEATURES = 128
CENTRE = 256
DIGIT = 64
MAGIC = 1.5 * 2.0**23

SINE = (4.440887881768876, -7.256453678610621, 3.2286686850204496)
COSINE = (1.414177779756007, -6.976808749845299, 5.708615924866348, -1.7132819288833234)


def horner(coefficients, u):
    value = coefficients[-1] * u + coefficients[-2]
    for coefficient in coefficients[-3::-1]:
        value = value * u + coefficient
    return value


def cos_sin(cycles):
    nearest = (cycles + MAGIC) - MAGIC
    r = cycles - nearest
    u = r * r
    half_sine = r * horner(SINE, u)
    half_cosine = horner(COSINE, u)
    return 1.0 - half_sine * half_sine, half_sine * half_cosine


def kernel(
    n, tile_b, tile_e,
    feat_ref, pos_ref, with_cos_ref, with_sin_ref, out_ref,
    phase, wcos, wsin, acc, sendbuf, recv, send_sem, recv_sem,
):
    me = lax.axis_index("blk")
    owned = out_ref.shape[0]
    beams, local = feat_ref.shape[0], pos_ref.shape[1]
    per_block = tile_b // owned
    blocks, tiles = beams // tile_b, local // tile_e
    home = me // per_block

    barrier = pltpu.get_barrier_semaphore()

    @pl.loop(1, n)
    def _(k):
        pl.semaphore_signal(
            barrier, inc=1, device_id={"blk": lax.rem(me + k, n)},
            device_id_type=pl.DeviceIdType.MESH,
        )

    def block_at(j):
        return lax.rem(home + 1 + j, blocks)

    def phase_dot(j, tile, slot):
        rows = pl.multiple_of(block_at(j) * tile_b, tile_b)
        columns = pl.multiple_of(tile * tile_e, tile_e)
        phase[slot] = jnp.dot(
            feat_ref[pl.ds(rows, tile_b), :], pos_ref[:, pl.ds(columns, tile_e)],
            preferred_element_type=jnp.float32,
        )

    def trig(slot):
        rows, columns = 32, 256
        for c in range(0, tile_e, columns):
            for r in range(0, tile_b, rows):
                cosine, sine = cos_sin(phase[slot, r:r + rows, c:c + columns])
                wcos[slot, r:r + rows, c:c + columns] = cosine.astype(jnp.bfloat16)
                wsin[slot, r:r + rows, c:c + columns] = sine.astype(jnp.bfloat16)

    def main_dot(tile, slot, acc_slot, first):
        at = pl.ds(pl.multiple_of(tile * tile_e, tile_e), tile_e)
        total = jnp.dot(wcos[slot], with_cos_ref[at, :], preferred_element_type=jnp.float32)
        total += jnp.dot(wsin[slot], with_sin_ref[at, :], preferred_element_type=jnp.float32)
        acc[acc_slot] = total if first else acc[acc_slot] + total

    def copy_to(owner):
        return pltpu.make_async_remote_copy(
            src_ref=sendbuf.at[pl.ds(pl.multiple_of(owner * owned, owned), owned), :],
            dst_ref=recv.at[me],
            send_sem=send_sem.at[owner],
            recv_sem=recv_sem.at[me],
            device_id={"blk": owner},
            device_id_type=pl.DeviceIdType.MESH,
        )

    def finish(j):
        block = block_at(j)
        rows = pl.multiple_of(block * tile_b, tile_b)
        sendbuf[pl.ds(rows, tile_b), :] = acc[lax.rem(j, 2)].astype(jnp.bfloat16)
        for k in range(per_block):
            owner = block * per_block + k

            @pl.when(owner != me)
            def _():
                copy_to(owner).start()

    wcos[1] = jnp.zeros_like(wcos[1])
    wsin[1] = jnp.zeros_like(wsin[1])
    acc[1] = jnp.zeros_like(acc[1])
    phase_dot(0, 0, 0)

    @pl.loop(0, blocks)
    def _(j):
        here, there = lax.rem(j, 2), lax.rem(j + 1, 2)
        phase_dot(j, 1, 1)
        trig(0)
        main_dot(tiles - 1, 1, there, False)
        if tiles > 2:
            phase_dot(j, 2, 0)
        else:
            phase_dot(j + 1, 0, 0)
        trig(1)
        main_dot(0, 0, here, True)

        @pl.when(j == 1)
        def _():
            pl.semaphore_wait(barrier, n - 1)

        @pl.when(j > 0)
        def _():
            finish(j - 1)

        @pl.loop(1, tiles // 2)
        def _(i):
            phase_dot(j, 2 * i + 1, 1)
            trig(0)
            main_dot(2 * i - 1, 1, here, False)
            last = (2 * i + 2 == tiles).astype(jnp.int32)
            phase_dot(j + last, (2 * i + 2) * (1 - last), 0)
            trig(1)
            main_dot(2 * i, 0, here, False)

    last_slot = (blocks - 1) % 2
    main_dot(tiles - 1, 1, last_slot, False)
    if blocks == 1:
        pl.semaphore_wait(barrier, n - 1)
    finish(blocks - 1)

    own = pl.multiple_of((me - home * per_block) * owned, owned)
    out_total = acc.at[last_slot]

    @pl.loop(1, n)
    def _(k):
        sender = lax.rem(me + n - k, n)
        pltpu.make_async_remote_copy(
            src_ref=sendbuf.at[pl.ds(0, owned), :],
            dst_ref=recv.at[sender],
            send_sem=send_sem.at[sender],
            recv_sem=recv_sem.at[sender],
            device_id={"blk": sender},
            device_id_type=pl.DeviceIdType.MESH,
        ).wait()
        at = pl.ds(own, owned)
        out_total[at, :] = out_total[at, :] + recv[sender].astype(jnp.float32)

    out_ref[...] = out_total[pl.ds(own, owned), :].astype(jnp.bfloat16)


def per_device(snapshots, bin_index, positions, directions, taper, beam_order):
    n = lax.axis_size("blk")
    _, local, parts, width = snapshots.shape
    elements, beams = positions.shape[1], directions.shape[1]
    owned = beams // n
    tile_b, tile_e = min(512, beams), min(512, local // 2)

    offset = lax.axis_index("blk") * local
    local_positions = lax.dynamic_slice_in_dim(positions, offset, local, 1)
    local_taper = lax.dynamic_slice_in_dim(taper, offset, local, 0)

    steps = jnp.take(directions, beam_order, axis=1) * bin_index[0]
    steps = ((steps + CYCLE // 2) & (CYCLE - 1)) - CYCLE // 2
    low = steps & (DIGIT - 1)
    high = steps - low
    shift = (jnp.sum(steps, axis=0, keepdims=True) * CENTRE) & (CYCLE - 1)
    features = jnp.concatenate([high, low, shift], axis=0).astype(jnp.float32) / CYCLE
    features = jnp.pad(features.astype(jnp.bfloat16), ((0, FEATURES - 7), (0, 0))).T
    centred = local_positions - CENTRE
    points = jnp.concatenate([centred, centred, jnp.ones_like(centred[:1])], axis=0)
    points = jnp.pad(points.astype(jnp.bfloat16), ((0, FEATURES - 7), (0, 0)))

    amplitude = (local_taper / math.sqrt(elements))[:, None]
    real = (snapshots[0, :, 0, :] * amplitude).astype(jnp.bfloat16)
    imag = (snapshots[0, :, 1, :] * amplitude).astype(jnp.bfloat16)
    with_cos = jnp.concatenate([real, imag], axis=1)
    with_sin = jnp.concatenate([imag, -real], axis=1)

    columns = parts * width
    vmem = pl.BlockSpec(memory_space=pltpu.VMEM)
    result = pl.pallas_call(
        functools.partial(kernel, n, tile_b, tile_e),
        out_shape=jax.ShapeDtypeStruct((owned, columns), jnp.bfloat16),
        in_specs=[vmem] * 4,
        out_specs=vmem,
        scratch_shapes=[
            pltpu.VMEM((2, tile_b, tile_e), jnp.float32),
            pltpu.VMEM((2, tile_b, tile_e), jnp.bfloat16),
            pltpu.VMEM((2, tile_b, tile_e), jnp.bfloat16),
            pltpu.VMEM((2, tile_b, columns), jnp.float32),
            pltpu.VMEM((beams, columns), jnp.bfloat16),
            pltpu.VMEM((n, owned, columns), jnp.bfloat16),
            pltpu.SemaphoreType.DMA((n,)),
            pltpu.SemaphoreType.DMA((n,)),
        ],
        compiler_params=pltpu.CompilerParams(collective_id=0, has_side_effects=True),
    )(features, points, with_cos, with_sin)
    return result.reshape(owned, 1, parts, width)


def solution(mesh):
    in_specs = (P("groups", "blk", None, None), P("groups"), P(), P(), P(), P())
    out_specs = P("blk", "groups", None, None)
    return jax.shard_map(
        per_device, mesh=mesh, in_specs=in_specs, out_specs=out_specs, check_vma=False
    )
```

time: 769 us -> 96.4 us (0.13)
  other arithmetic: 587 us -> 5.75 us
  waiting for transfers between devices: 64.7 us -> 0 us
  Pallas kernels: 0 us -> 63.5 us
  local copies, waits for them, and re-layouts: 76.8 us -> 25.5 us
  matrix products: 25.3 us -> 0 us
  between operations: 13.4 us -> 0.75 us
    dot_general x16 -> x0, other arithmetic: 583 us -> none  [the longest x8 292 us: beam_terms(): with_imag = jnp.dot(weight_im, columns, preferred_element_type=jnp.float32)]
    reduce_scatter x1 -> x0, waiting for transfers between devices: 64.7 us -> none  [per_device(): lax.psum_scatter(blocked_terms(ordered, local_positions, local_taper, sna...]
    pallas_call x0 -> x1, Pallas kernels: none -> 63.5 us  [per_device(): pl.pallas_call(functools.partial(kernel, n, tile_b, tile_e), out_shape=ja...]
    dynamic_update_slice x16 -> x0, local copies, waits for them, and re-layouts: 52.9 us -> none  [blocked_terms(): result = lax.map(per_block, blocks)]
    dot_general x16 -> x0, matrix products: 25.3 us -> none  [the longest x8 12.7 us: beam_terms(): with_imag = jnp.dot(weight_im, columns, preferred_element_type=jnp.float32)]
  transfers between devices with their start and end apart: 1 -> 0, of which waited for: 1 -> 0; matrix products, arithmetic and copies ran while one was open for 0% -> 0% of each run, Pallas kernels for 0% -> 0%
where the time goes in v1:
time: 96.4 us; the launch traced here: 95.5 us
  Pallas kernels  63.5 us (66%)
  local copies, waits for them, and re-layouts  25.5 us (26%)
  other arithmetic  5.75 us (6%)
    pallas_call x1, Pallas kernels, per_device(): pl.pallas_call(functools.partial(kernel, n, tile_b, tile_e), out_shape=ja...  63.5 us
    gather x2, local copies, waits for them, and re-layouts, per_device(): steps = jnp.take(directions, beam_order, axis=1) * bin_index[0]  16.3 us
    unnamed x7, local copies, waits for them, and re-layouts  2.7 us
    concatenate x1, other arithmetic, per_device(): with_sin = jnp.concatenate([imag, -real], axis=1)  2.46 us
    slice x1, local copies, waits for them, and re-layouts, per_device(): real = (snapshots[0, :, 0, :] * amplitude).astype(jnp.bfloat16)  2.07 us

profile of v1, /device:TPU:0, one launch (start us, length us, event | category | flops | bytes accessed | tf_op | source)
XLA Modules:
  0.0 95.5 jit_solution(8084612821621972670)
XLA Ops:
  0.0 0.7 dynamic-slice_multiply_fusion
  0.7 2.1 %fusion.8 = (bf16[1,4096,1,64]{1,3,2,0:T(8,128)(2,1)S(1)}, bf16[1,4096,1,64]{1,3,2,0:T(8,128)(2,1)}) fusion(bf16[1,4096,2,64]{1,3,2,0:T(8,128)(2,1)} %param.6), kind=kLoop, calls=%fused_computation.23 | loop fusion | bytes 2097152 | tf_op jit(solution)/shard_map/slice | solution.py:189
  2.8 0.5 copy.30
  3.3 0.7 fusion.6
  4.0 1.5 %copy.31 = bf16[1,4096,1,64]{3,1,2,0:T(8,128)(2,1)S(1)} copy(bf16[1,4096,1,64]{1,3,2,0:T(8,128)(2,1)} %get-tuple-element.10) | data formatting | bytes 1048576
  5.5 0.7 fusion
  6.2 0.0 copy-start
  6.3 2.5 %pad_maximum_fusion.1 = (bf16[4096,128]{1,0:T(8,128)(2,1)}, bf16[4096,128]{1,0:T(8,128)(2,1)}) fusion(bf16[4096,64]{1,0:T(8,128)(2,1)S(1)} %get-tuple-element.5, bf16[4096,64]{1,0:T(8,128)(2,1)S(1)} %fusion, bf16[4096,64]{1,0:T(8,128)(2,1)S(1)} %get-tuple-element.6), kind=kLoop, calls=%fused_computation.6 | loop fusion | flops 4194304 | bytes 3670016 | tf_op jit(solution)/shard_map/concatenate | solution.py:192
  8.7 0.0 copy-start.1
  8.7 0.0 copy-done
  8.7 0.6 copy.24
  9.4 0.1 copy-done.1
  9.4 14.1 %gather_fusion = s32[4096,3]{1,0:T(8,128)} fusion(s32[3,4096]{0,1:T(8,128)S(1)} %copy.24, s32[4096]{0:T(1024)S(1)} %fusion.4), kind=kCustom, calls=%fused_computation | custom fusion | bytes 114688 | tf_op jit(solution)/shard_map/jit(_take)/gather | solution.py:177
  23.5 2.2 %copy.25 = s32[4096,3]{0,1:T(4,128)S(1)} copy(s32[4096,3]{1,0:T(8,128)} %gather_fusion) | data formatting | bytes 98304 | tf_op jit(solution)/shard_map/jit(_take)/gather | solution.py:177
  26.5 0.1 fusion.5
  26.5 0.1 fusion.3
  26.6 0.5 copy.26
  27.1 1.2 %pad_bitcast_fusion.feat_ref = bf16[4096,128]{1,0:T(8,128)(2,1)} fusion(bf16[7,4096]{0,1:T(8,128)(2,1)S(1)} %copy.26), kind=kLoop, calls=%fused_computation.7 | loop fusion | bytes 1105920 | tf_op jit(solution)/shard_map/transpose | solution.py:183
  28.3 0.9 add_convert_fusion.1
  29.2 0.1 pad.15.clone
  29.2 0.1 maximum_maximum_fusion
  29.3 1.1 %pad.8.pos_ref = bf16[128,4096]{1,0:T(8,128)(2,1)} pad(bf16[7,4096]{1,0:T(8,128)(2,1)S(1)} %maximum_maximum_fusion, bf16[]{:T(256)} %constant.42.clone.1), padding=0_121x0_0 | pad | bytes 1105922 | tf_op jit(solution)/shard_map/jit(_pad)/pad | solution.py:186
  30.4 63.5 %shard_map.64 = bf16[256,128]{1,0:T(8,128)(2,1)} custom-call(bf16[4096,128]{1,0:T(8,128)(2,1)} %pad_bitcast_fusion.feat_ref, bf16[128,4096]{1,0:T(8,128)(2,1)} %pad.8.pos_ref, bf16[4096,128]{1,0:T(8,128)(2,1)} %get-tuple-element.8.with_cos_ref, bf16[4096,128]{1,0:T(8,128)(2,1)} %get-tuple-element.7.with_sin_ref), custom_call_target="tpu_custom_call" | custom-call | tf_op jit(solution)/shard_map/pallas_call | solution.py:196
  93.9 1.6 %copy.29 = bf16[256,128]{0,1:T(8,128)(2,1)} copy(bf16[256,128]{1,0:T(8,128)(2,1)} %shard_map.64) | data formatting | bytes 131072 | tf_op jit(solution)/shard_map/pallas_call | solution.py:196
  (4 shorter events, 0.1 us)
Async XLA Ops:
  6.2 2.5 %copy-start = (s32[3,4096]{1,0:T(4,128)S(1)}, s32[3,4096]{1,0:T(4,128)}, u32[]{:S(2)}) copy-start(s32[3,4096]{1,0:T(4,128)} %param.9) | copy-start | bytes 147460
  8.7 0.7 copy-start.1

commit v2 on v1

--- a/solution.py
+++ b/solution.py
@@ -10,9 +10,9 @@
 
 CYCLE = 8192
 FEATURES = 128
+LANES = 128
 CENTRE = 256
 DIGIT = 64
-MAGIC = 1.5 * 2.0**23
 
 SINE = (4.440887881768876, -7.256453678610621, 3.2286686850204496)
 COSINE = (1.414177779756007, -6.976808749845299, 5.708615924866348, -1.7132819288833234)
@@ -26,7 +26,7 @@
 
 
 def cos_sin(cycles):
-    nearest = (cycles + MAGIC) - MAGIC
+    nearest = jnp.round(cycles)
     r = cycles - nearest
     u = r * r
     half_sine = r * horner(SINE, u)
@@ -34,17 +34,87 @@
     return 1.0 - half_sine * half_sine, half_sine * half_cosine
 
 
+def dot_rows(a, b):
+    return lax.dot_general(a, b, (((1,), (1,)), ((), ())), preferred_element_type=jnp.float32)
+
+
+def build_features(bin_value, direction_ref, order_ref, table, feat_ref):
+    beams = direction_ref.shape[1]
+    groups = beams // LANES
+    table[...] = jnp.zeros_like(table)
+    for h in range(groups):
+        columns = direction_ref[:, h * LANES:(h + 1) * LANES].astype(jnp.float32)
+        table[8 * h:8 * h + 3, :] = columns
+    chunk = min(512, beams)
+
+    @pl.loop(0, beams // chunk)
+    def _(i):
+        at = pl.ds(pl.multiple_of(i * chunk, chunk), chunk)
+        order = order_ref[:, at]
+        row = lax.broadcasted_iota(jnp.int32, (LANES, chunk), 0)
+        hot = jnp.where(row == (order & (LANES - 1)), 1.0, 0.0).astype(jnp.bfloat16)
+        picked = jnp.dot(table[...].astype(jnp.bfloat16), hot, preferred_element_type=jnp.float32)
+        block = jnp.broadcast_to(order // LANES, (8, chunk))
+        ordered = jnp.zeros((8, chunk), jnp.float32)
+        for h in range(groups):
+            ordered = jnp.where(block == h, picked[8 * h:8 * h + 8, :], ordered)
+        steps = ordered.astype(jnp.int32) * bin_value
+        steps = ((steps + CYCLE // 2) & (CYCLE - 1)) - CYCLE // 2
+        low = steps & (DIGIT - 1)
+        high = steps - low
+        shift = ((steps[0:1] + steps[1:2] + steps[2:3]) * CENTRE) & (CYCLE - 1)
+        row = lax.broadcasted_iota(jnp.int32, (8, chunk), 0)
+        high = jnp.where(row == 3, jnp.broadcast_to(shift, (8, chunk)), high)
+        zeros = jnp.zeros((FEATURES - 16, chunk), jnp.float32)
+        scale = 1.0 / CYCLE
+        features = jnp.concatenate(
+            [high.astype(jnp.float32) * scale, low.astype(jnp.float32) * scale, zeros], axis=0
+        )
+        feat_ref[at, :] = features.T.astype(jnp.bfloat16)
+
+
+def build_points(position_ref, raised, pos_ref):
+    raised[...] = jnp.zeros_like(raised)
+    raised[0:3, :] = (position_ref[...] - CENTRE).astype(jnp.float32)
+    raised[3:4, :] = jnp.ones((1, raised.shape[1]), jnp.float32)
+    pos_ref[...] = jnp.zeros_like(pos_ref)
+    pos_ref[0:16, :] = jnp.concatenate([raised[...], raised[...]], axis=0).astype(jnp.bfloat16)
+
+
+def scale_snapshots(scale, snap_ref, taper_ref, with_cos_ref, with_sin_ref):
+    width, local = snap_ref.shape[0] // 2, snap_ref.shape[1]
+    chunk = min(512, local)
+
+    @pl.loop(0, local // chunk)
+    def _(i):
+        at = pl.ds(pl.multiple_of(i * chunk, chunk), chunk)
+        amplitude = jnp.broadcast_to(taper_ref[:, at] * scale, (width, chunk))
+        real = snap_ref[0:width, at].astype(jnp.float32) * amplitude
+        imag = snap_ref[width:2 * width, at].astype(jnp.float32) * amplitude
+        with_cos_ref[0:width, at] = real.astype(jnp.bfloat16)
+        with_cos_ref[width:2 * width, at] = imag.astype(jnp.bfloat16)
+        with_sin_ref[0:width, at] = imag.astype(jnp.bfloat16)
+        with_sin_ref[width:2 * width, at] = (-real).astype(jnp.bfloat16)
+
+
 def kernel(
     n, tile_b, tile_e,
-    feat_ref, pos_ref, with_cos_ref, with_sin_ref, out_ref,
-    phase, wcos, wsin, acc, sendbuf, recv, send_sem, recv_sem,
+    bin_ref, snap_ref, position_hbm, direction_ref, taper_hbm, order_ref, out_ref,
+    position_ref, taper_ref, raised, table, feat_ref, pos_ref, with_cos_ref, with_sin_ref,
+    phase, wcos, wsin, acc, sendbuf, recv, final, copy_sem, send_sem, recv_sem,
 ):
     me = lax.axis_index("blk")
-    owned = out_ref.shape[0]
+    owned = out_ref.shape[1]
     beams, local = feat_ref.shape[0], pos_ref.shape[1]
     per_block = tile_b // owned
     blocks, tiles = beams // tile_b, local // tile_e
     home = me // per_block
+
+    mine = pl.ds(pl.multiple_of(me * local, local), local)
+    fetch_positions = pltpu.make_async_copy(position_hbm.at[:, mine], position_ref, copy_sem.at[0])
+    fetch_taper = pltpu.make_async_copy(taper_hbm.at[:, mine], taper_ref, copy_sem.at[1])
+    fetch_positions.start()
+    fetch_taper.start()
 
     barrier = pltpu.get_barrier_semaphore()
 
@@ -54,6 +124,13 @@
             barrier, inc=1, device_id={"blk": lax.rem(me + k, n)},
             device_id_type=pl.DeviceIdType.MESH,
         )
+
+    build_features(bin_ref[0], direction_ref, order_ref, table, feat_ref)
+    fetch_positions.wait()
+    build_points(position_ref, raised, pos_ref)
+    fetch_taper.wait()
+    scale = 1.0 / math.sqrt(position_hbm.shape[1])
+    scale_snapshots(scale, snap_ref, taper_ref, with_cos_ref, with_sin_ref)
 
     def block_at(j):
         return lax.rem(home + 1 + j, blocks)
@@ -76,8 +153,8 @@
 
     def main_dot(tile, slot, acc_slot, first):
         at = pl.ds(pl.multiple_of(tile * tile_e, tile_e), tile_e)
-        total = jnp.dot(wcos[slot], with_cos_ref[at, :], preferred_element_type=jnp.float32)
-        total += jnp.dot(wsin[slot], with_sin_ref[at, :], preferred_element_type=jnp.float32)
+        total = dot_rows(wcos[slot], with_cos_ref[:, at])
+        total += dot_rows(wsin[slot], with_sin_ref[:, at])
         acc[acc_slot] = total if first else acc[acc_slot] + total
 
     def copy_to(owner):
@@ -160,7 +237,10 @@
         at = pl.ds(own, owned)
         out_total[at, :] = out_total[at, :] + recv[sender].astype(jnp.float32)
 
-    out_ref[...] = out_total[pl.ds(own, owned), :].astype(jnp.bfloat16)
+    if owned < final.shape[0]:
+        final[...] = jnp.zeros_like(final)
+    final[0:owned, :] = out_total[pl.ds(own, owned), :]
+    out_ref[...] = final[...].T[:, 0:owned].astype(jnp.bfloat16)
 
 
 def per_device(snapshots, bin_index, positions, directions, taper, beam_order):
@@ -170,47 +250,41 @@
     owned = beams // n
     tile_b, tile_e = min(512, beams), min(512, local // 2)
 
-    offset = lax.axis_index("blk") * local
-    local_positions = lax.dynamic_slice_in_dim(positions, offset, local, 1)
-    local_taper = lax.dynamic_slice_in_dim(taper, offset, local, 0)
-
-    steps = jnp.take(directions, beam_order, axis=1) * bin_index[0]
-    steps = ((steps + CYCLE // 2) & (CYCLE - 1)) - CYCLE // 2
-    low = steps & (DIGIT - 1)
-    high = steps - low
-    shift = (jnp.sum(steps, axis=0, keepdims=True) * CENTRE) & (CYCLE - 1)
-    features = jnp.concatenate([high, low, shift], axis=0).astype(jnp.float32) / CYCLE
-    features = jnp.pad(features.astype(jnp.bfloat16), ((0, FEATURES - 7), (0, 0))).T
-    centred = local_positions - CENTRE
-    points = jnp.concatenate([centred, centred, jnp.ones_like(centred[:1])], axis=0)
-    points = jnp.pad(points.astype(jnp.bfloat16), ((0, FEATURES - 7), (0, 0)))
-
-    amplitude = (local_taper / math.sqrt(elements))[:, None]
-    real = (snapshots[0, :, 0, :] * amplitude).astype(jnp.bfloat16)
-    imag = (snapshots[0, :, 1, :] * amplitude).astype(jnp.bfloat16)
-    with_cos = jnp.concatenate([real, imag], axis=1)
-    with_sin = jnp.concatenate([imag, -real], axis=1)
-
     columns = parts * width
+    lanes_last = snapshots[0].transpose(1, 2, 0).reshape(columns, local)
+    hbm = pl.BlockSpec(memory_space=pl.ANY)
     vmem = pl.BlockSpec(memory_space=pltpu.VMEM)
     result = pl.pallas_call(
         functools.partial(kernel, n, tile_b, tile_e),
-        out_shape=jax.ShapeDtypeStruct((owned, columns), jnp.bfloat16),
-        in_specs=[vmem] * 4,
+        out_shape=jax.ShapeDtypeStruct((columns, owned), jnp.bfloat16),
+        in_specs=[pl.BlockSpec(memory_space=pltpu.SMEM), vmem, hbm, vmem, hbm, vmem],
         out_specs=vmem,
         scratch_shapes=[
+            pltpu.VMEM((3, local), jnp.int32),
+            pltpu.VMEM((1, local), jnp.float32),
+            pltpu.VMEM((8, local), jnp.float32),
+            pltpu.VMEM((8 * (beams // LANES), LANES), jnp.float32),
+            pltpu.VMEM((beams, FEATURES), jnp.bfloat16),
+            pltpu.VMEM((FEATURES, local), jnp.bfloat16),
+            pltpu.VMEM((columns, local), jnp.bfloat16),
+            pltpu.VMEM((columns, local), jnp.bfloat16),
             pltpu.VMEM((2, tile_b, tile_e), jnp.float32),
             pltpu.VMEM((2, tile_b, tile_e), jnp.bfloat16),
             pltpu.VMEM((2, tile_b, tile_e), jnp.bfloat16),
             pltpu.VMEM((2, tile_b, columns), jnp.float32),
             pltpu.VMEM((beams, columns), jnp.bfloat16),
             pltpu.VMEM((n, owned, columns), jnp.bfloat16),
+            pltpu.VMEM((max(owned, LANES), columns), jnp.float32),
+            pltpu.SemaphoreType.DMA((2,)),
             pltpu.SemaphoreType.DMA((n,)),
             pltpu.SemaphoreType.DMA((n,)),
         ],
         compiler_params=pltpu.CompilerParams(collective_id=0, has_side_effects=True),
-    )(features, points, with_cos, with_sin)
-    return result.reshape(owned, 1, parts, width)
+    )(
+        bin_index, lanes_last, positions, directions,
+        taper.reshape(1, elements), beam_order.reshape(1, beams),
+    )
+    return result.reshape(1, parts, width, owned).transpose(3, 0, 1, 2)
 
 
 def solution(mesh):

time: 96.4 us -> 66.2 us (0.69)
  local copies, waits for them, and re-layouts: 25.5 us -> 1.47 us
  other arithmetic: 5.75 us -> 0 us
    gather x2 -> x0, local copies, waits for them, and re-layouts: 16.3 us -> none  [per_device(): steps = jnp.take(directions, beam_order, axis=1) * bin_index[0]]
    concatenate x2 -> x0, other arithmetic: 2.55 us -> none  [the longest x1 2.46 us: per_device(): with_sin = jnp.concatenate([imag, -real], axis=1)]
    slice x1 -> x0, local copies, waits for them, and re-layouts: 2.07 us -> none  [per_device(): real = (snapshots[0, :, 0, :] * amplitude).astype(jnp.bfloat16)]
    pallas_call x1 -> x0, local copies, waits for them, and re-layouts: 1.57 us -> none  [per_device(): pl.pallas_call(functools.partial(kernel, n, tile_b, tile_e), out_shape=ja...]
    unnamed x7 -> x1, local copies, waits for them, and re-layouts: 2.7 us -> 1.47 us
    transpose x1 -> x0, local copies, waits for them, and re-layouts: 1.17 us -> none  [per_device(): jnp.pad(features.astype(jnp.bfloat16), ((0, FEATURES - 7), (0, 0)))]
    pad x1 -> x0, local copies, waits for them, and re-layouts: 1.12 us -> none  [per_device(): points = jnp.pad(points.astype(jnp.bfloat16), ((0, FEATURES - 7), (0, 0)))]
where the time goes in v2:
time: 66.2 us; the launch traced here: 65.6 us
  Pallas kernels  63.5 us (96%)
  local copies, waits for them, and re-layouts  1.47 us (2%)
    pallas_call x1, Pallas kernels, per_device(): pl.pallas_call(functools.partial(kernel, n, tile_b, tile_e), out_shape=ja...  63.5 us
    unnamed x1, local copies, waits for them, and re-layouts  1.47 us

profile of v2, /device:TPU:0, one launch (start us, length us, event | category | flops | bytes accessed | tf_op | source)
XLA Modules:
  0.0 65.6 jit_solution(7636027583729003572)
XLA Ops:
  0.7 63.5 %shard_map.64 = bf16[128,256]{1,0:T(8,128)(2,1)} custom-call(s32[1]{0:T(128)S(6)} %copy.8.bin_ref, bf16[128,4096]{1,0:T(8,128)(2,1)} %bitcast.10, s32[3,65536]{1,0:T(4,128)} %position_hbm.1, s32[3,4096]{1,0:T(4,128)} %direction_ref.1, f32[1,65536]{1,0:T(1,128)} %bitcast.12, s32[1,4096]{1,0:T(1,128)} %bitcast.13), custom_call_target="tpu_custom_call" | custom-call | tf_op jit(solution)/shard_map/pallas_call | solution.py:257
  64.1 1.5 %copy.9 = bf16[256,1,2,64]{0,3,2,1:T(8,128)(2,1)} copy(bf16[256,1,2,64]{0,3,2,1:T(8,128)(2,1)} %bitcast.11) | data formatting | bytes 131072
